TPU v7x, 32 devices: a whole 2x2x4 slice. The times are simulated.
32 devices in a mesh: rep: 4 (over x, y), dp: 8 (over z, core).
Axes of the slice: x: 2, y: 2, z: 4, core: 2. Of those that a mesh axis runs over, the one named last changes fastest.
Arguments:
- a: bfloat16 [32, 4, 8192, 768], P(('rep', 'dp')), parts along dimension 0
- g: bfloat16 [32, 4, 8192, 3072], P(('rep', 'dp')), parts along dimension 0
Outputs:
- output: bfloat16 [16, 768, 3072], P('rep'), parts along dimension 0
There are 4 independent parts. A program takes and returns all parts, laid end to end along the dimension named above; each array names one.
All inputs are finite; a program needn't handle non-finite values.
Results may differ from a plain program's by a relative error of at most 0.012.
Values are sent between devices in bfloat16 or wider.
A program may use at most 2 GiB of HBM per device.

v0:
```python
import jax
import jax.numpy as jnp


def solution(mesh):
    groups = mesh.shape["rep"]

    def step(a, g):
        a, g = (t.reshape(groups, -1, *t.shape[1:]) for t in (a, g))
        sums = jnp.einsum("rsntd,rsntf->rndf", a, g, preferred_element_type=jnp.float32)
        return sums.astype(jnp.bfloat16).reshape(-1, *sums.shape[2:])

    return step
```

profile of v0, /device:TPU:0, one launch (start us, length us, event | category | flops | bytes accessed | tf_op | source)
XLA Modules:
  0.0 901.7 jit_solution(1050066570870277509)
XLA Ops:
  0.0 169.3 %fusion.3 = f32[1,4,768,3072]{3,2,1,0:T(8,128)} fusion(bf16[1,4,8192,3072]{3,2,1,0:T(8,128)(2,1)} %param.1, bf16[1,4,8192,768]{3,2,1,0:T(8,128)(2,1)} %param), kind=kOutput, calls=%fused_computation.4 | convolution fusion | flops 154618822656 | bytes 289406976 | tf_op jit(solution)/rsntd,rsntf->rndf/dot_general | solution.py:10
  169.3 732.4 %all-reduce.2 = bf16[1,4,768,3072]{3,2,1,0:T(8,128)(2,1)} all-reduce(f32[1,4,768,3072]{3,2,1,0:T(8,128)} %fusion.3), channel_id=1, replica_groups=[4,8]<=[32], use_global_device_ids=true, to_apply=%add.clone | all-reduce | flops 9437184 | bytes 56623104 | tf_op jit(solution)/rsntd,rsntf->rndf/dot_general | solution.py:10
where the time goes:
time: 902 us
  blocking collectives  732 us (81%)
  matrix products  169 us (19%)
    dot_general x1, blocking collectives, step(): jnp.einsum('rsntd,rsntf->rndf', a, g, preferred_element_type=jnp.float32)  732 us
    dot_general x1, matrix products, step(): jnp.einsum('rsntd,rsntf->rndf', a, g, preferred_element_type=jnp.float32)  169 us

commit v1 on v0

v1 whole, which is shorter than its diff:
```python
import functools

import jax
import jax.numpy as jnp
from jax import lax
from jax.experimental import pallas as pl
from jax.experimental.pallas import tpu as pltpu
from jax.sharding import PartitionSpec as P

MESH = pl.DeviceIdType.MESH
FB = 512
UB = 256
NK = 2
GS = 3
R = 8
LC, LD, LE = 3, 5, 7
KEEP = 6


def kernel(
    a, g, out, abuf, gbuf, acc, own, sib_out, sib_in, low_out, low_in, pair_out, pair_in, fin,
    a_sem, g_sem, sib_s, sib_r, low_s, low_r, pair_s, pair_r, fin_s, fin_r, put_s, loc_s, put_r,
):
    n_mat, tokens, rows = a.shape
    cols = g.shape[2]
    kc, half = tokens // NK, rows // 2
    per_mat = cols // FB
    steps = n_mat * per_mat
    units, prods = 2 * steps, NK * steps

    me = lax.axis_index("dp")
    z, core = me // 2, me % 2
    middle = (z + 1) // 2 == 1
    sibling = z * 2 + 1 - core
    partner = (z + 1 - 2 * (z % 2)) * 2 + core
    across = (3 - z) * 2 + core
    mine = pl.multiple_of(core * half, half)
    other = pl.multiple_of((1 - core) * half, half)

    def a_copy(n, k):
        return pltpu.make_async_copy(
            a.at[n, pl.ds(k * kc, kc)], abuf.at[n % 2, pl.ds(k * kc, kc)], a_sem.at[n % 2, k]
        )

    def g_copy(t):
        n, j, k = t // (per_mat * NK), (t // NK) % per_mat, t % NK
        return pltpu.make_async_copy(
            g.at[n, pl.ds(pl.multiple_of(k * kc, kc), kc), pl.ds(pl.multiple_of(j * FB, FB), FB)],
            gbuf.at[t % GS],
            g_sem.at[t % GS],
        )

    def place(u):
        n, col = u // (2 * per_mat), u % (2 * per_mat)
        return out.at[n, pl.ds(mine, half), pl.ds(pl.multiple_of(col * UB, UB), UB)]

    def send(src, dst, s, r, device):
        return pltpu.make_async_remote_copy(
            src_ref=src, dst_ref=dst, send_sem=s, recv_sem=r, device_id={"dp": device}, device_id_type=MESH
        )

    def sib_copy(u):
        return send(sib_out.at[u % 4], sib_in.at[u % 4], sib_s.at[u % 4], sib_r.at[u % 4], sibling)

    def low_copy(u):
        return send(low_out.at[u % R], low_in.at[u % R], low_s.at[u % R], low_r.at[u % R], partner)

    def pair_copy(u):
        return send(pair_out.at[u % R], pair_in.at[u % R], pair_s.at[u % R], pair_r.at[u % R], across)

    def fin_copy(u):
        return send(fin.at[u % R], place(u), fin_s.at[u % R], fin_r.at[u % R], partner)

    def loc_copy(u):
        return pltpu.make_async_copy(fin.at[u % R], place(u), loc_s.at[u % R])

    def put_copy(u):
        return send(fin.at[u % R], place(u), put_s.at[u % R], put_r.at[u], sibling)

    def pass_copy(u):
        return send(place(u), place(u), put_s.at[u % R], put_r.at[u], sibling)

    for k in range(NK):
        a_copy(0, k).start()
        g_copy(jnp.int32(k)).start()

    barrier = pltpu.get_barrier_semaphore()
    for d in (sibling, partner):
        pl.semaphore_signal(barrier, inc=1, device_id={"dp": d}, device_id_type=MESH)

    @pl.when(middle)
    def _():
        pl.semaphore_signal(barrier, inc=1, device_id={"dp": across}, device_id_type=MESH)
        pl.semaphore_wait(barrier, 3)

    @pl.when(jnp.logical_not(middle))
    def _():
        pl.semaphore_wait(barrier, 2)

    def product(t):
        n, j, k = t // (per_mat * NK), (t // NK) % per_mat, t % NK

        @pl.when(t + GS - 1 < prods)
        def _():
            g_copy(t + GS - 1).start()

        @pl.when(j == 0)
        def _():
            a_copy(n, k).wait()

        @pl.when((j == 1) & (n < n_mat - 1))
        def _():
            a_copy(n + 1, k).start()

        g_copy(t).wait()
        d = lax.dot_general(
            abuf[n % 2, pl.ds(pl.multiple_of(k * kc, kc), kc), :],
            gbuf[t % GS],
            (((0,), (0,)), ((), ())),
            preferred_element_type=jnp.float32,
        )

        @pl.when(k == 0)
        def _():
            acc[...] = d

        @pl.when(k > 0)
        def _():
            acc[...] += d

    def stage_a(i):
        for h in range(2):
            u, c = 2 * i + h, slice(h * UB, (h + 1) * UB)
            sib_out[u % 4] = acc[pl.ds(other, half), c].astype(jnp.bfloat16)
            sib_copy(u).start()
        for h in range(2):
            u, c = 2 * i + h, slice(h * UB, (h + 1) * UB)
            own[u % R] = acc[pl.ds(mine, half), c]

    def stage_b(u):
        sib_copy(u).wait()
        total = own[u % R] + sib_in[u % 4].astype(jnp.float32)

        @pl.when(middle)
        def _():
            own[u % R] = total

        @pl.when(jnp.logical_not(middle))
        def _():
            low_out[u % R] = total.astype(jnp.bfloat16)
            low_copy(u).start()

    def stage_c(u):
        low_copy(u).wait_recv()
        pair_out[u % R] = (own[u % R] + low_in[u % R].astype(jnp.float32)).astype(jnp.bfloat16)
        pair_copy(u).start()

    def stage_d(u):
        @pl.when(u >= KEEP)
        def _():
            finish_d(u - KEEP)

        pair_copy(u).wait()
        fin[u % R] = (pair_out[u % R].astype(jnp.float32) + pair_in[u % R].astype(jnp.float32)).astype(jnp.bfloat16)
        fin_copy(u).start()
        put_copy(u).start()
        loc_copy(u).start()

    def finish_d(u):
        fin_copy(u).wait_send()
        put_copy(u).wait_send()
        loc_copy(u).wait()

    def stage_e(u):
        @pl.when(u >= KEEP)
        def _():
            pass_copy(u - KEEP).wait_send()

        low_copy(u).wait_send()
        fin_copy(u).wait_recv()
        pass_copy(u).start()

    def within(u):
        return (u >= 0) & (u < units)

    def tick(t, carry):
        i, k = t // 2, t % 2

        @pl.when(t < prods)
        def _():
            product(t)

            @pl.when(k == 1)
            def _():
                stage_a(i)

        @pl.when((k == 0) & within(t - 2))
        def _():
            stage_b(t - 2)
            stage_b(t - 1)

        @pl.when(middle & within(t - LC))
        def _():
            stage_c(t - LC)

        @pl.when(middle & within(t - LD))
        def _():
            stage_d(t - LD)

        @pl.when(jnp.logical_not(middle) & within(t - LE))
        def _():
            stage_e(t - LE)

        return carry

    lax.fori_loop(0, units + LE, tick, 0)

    @pl.when(middle)
    def _():
        lax.fori_loop(units - KEEP, units, lambda u, c: (finish_d(u), c)[1], 0)

    @pl.when(jnp.logical_not(middle))
    def _():
        lax.fori_loop(units - KEEP, units, lambda u, c: (pass_copy(u).wait_send(), c)[1], 0)

    def sibling_rows(u, c):
        put_copy(u).wait_recv()
        return c

    lax.fori_loop(0, units, sibling_rows, 0)


def local(a, g):
    a, g = a[0], g[0]
    n_mat, tokens, rows = a.shape
    cols = g.shape[2]
    kc, half = tokens // NK, rows // 2
    steps = n_mat * (cols // FB)
    bf, f32 = jnp.bfloat16, jnp.float32
    ring = pltpu.VMEM((R, half, UB), bf)
    four = pltpu.VMEM((4, half, UB), bf)
    dma = pltpu.SemaphoreType.DMA
    return pl.pallas_call(
        kernel,
        out_shape=jax.ShapeDtypeStruct((n_mat, rows, cols), bf),
        in_specs=[pl.BlockSpec(memory_space=pl.ANY)] * 2,
        out_specs=pl.BlockSpec(memory_space=pl.ANY),
        scratch_shapes=[
            pltpu.VMEM((2, tokens, rows), bf),
            pltpu.VMEM((GS, kc, FB), bf),
            pltpu.VMEM((rows, FB), f32),
            pltpu.VMEM((R, half, UB), f32),
            four, four, ring, ring, ring, ring, ring,
            dma((2, NK)), dma((GS,)),
            dma((4,)), dma((4,)), dma((R,)), dma((R,)), dma((R,)), dma((R,)),
            dma((R,)), dma((R,)), dma((R,)), dma((R,)), dma((2 * steps,)),
        ],
        compiler_params=pltpu.CompilerParams(
            collective_id=0, has_side_effects=True, vmem_limit_bytes=64_000_000
        ),
    )(a, g)


def solution(mesh):
    assert mesh.shape["dp"] == 8
    both = ("rep", "dp")
    return jax.shard_map(
        local, mesh=mesh, in_specs=(P(both), P(both)), out_specs=P("rep"), check_vma=False
    )
```

time: 902 us -> 254 us (0.28)
  blocking collectives: 732 us -> 0 us
  Pallas kernels: 0 us -> 237 us
  matrix products: 169 us -> 0 us
  local copies, waits for them, and re-layouts: 0 us -> 16.7 us
    dot_general x1 -> x0, blocking collectives: 732 us -> none  [step(): jnp.einsum('rsntd,rsntf->rndf', a, g, preferred_element_type=jnp.float32)]
    pallas_call x0 -> x1, Pallas kernels: none -> 237 us  [local(): pl.pallas_call(kernel, out_shape=jax.ShapeDtypeStruct((n_mat, rows, cols)...]
    dot_general x1 -> x0, matrix products: 169 us -> none  [step(): jnp.einsum('rsntd,rsntf->rndf', a, g, preferred_element_type=jnp.float32)]
    unnamed x0 -> x1, local copies, waits for them, and re-layouts: none -> 16.7 us
where the time goes in v1:
time: 254 us; the launch traced here: 253 us
  Pallas kernels  237 us (93%)
  local copies, waits for them, and re-layouts  16.7 us (7%)
    pallas_call x1, Pallas kernels, local(): pl.pallas_call(kernel, out_shape=jax.ShapeDtypeStruct((n_mat, rows, cols)...  237 us
    unnamed x1, local copies, waits for them, and re-layouts  16.7 us

profile of v1, /device:TPU:0, one launch (start us, length us, event | category | flops | bytes accessed | tf_op | source)
XLA Modules:
  0.0 253.3 jit_solution(9190602266983105831)
XLA Ops:
  0.0 236.6 %shard_map.28 = bf16[4,768,3072]{2,1,0:T(8,128)(2,1)} custom-call(bf16[4,8192,768]{2,1,0:T(8,128)(2,1)} %bitcast.2, bf16[4,8192,3072]{2,1,0:T(8,128)(2,1)} %bitcast.1.g), custom_call_target="tpu_custom_call" | custom-call | tf_op jit(solution)/shard_map/pallas_call | solution.py:243
  236.6 16.7 %copy.4 = bf16[4,768,3072]{2,1,0:T(8,128)(2,1)} copy(bf16[4,768,3072]{2,1,0:T(8,128)(2,1)} %shard_map.28) | data formatting | bytes 37748736

commit v2 on v0

v2 whole, which is shorter than its diff:
```python
import jax
import jax.numpy as jnp
from jax import lax
from jax.experimental import pallas as pl
from jax.experimental.pallas import tpu as pltpu
from jax.sharding import PartitionSpec as P

MESH = pl.DeviceIdType.MESH
FB = 512
UB = 256
Q = 2
R = 10
S = 8
LC, LD, LE = 2, 4, 9
KEEP = 6
NP = 6
PC, PD = 4, 7
OWN = 4


def kernel(
    a, g, out, abuf, gbuf, own, sib_out, sib_in, low, pair_out, pair_in, fin,
    a_sem, g_sem, sib_s, sib_r, low_s, low_r, pair_s, pair_r, fin_s, fin_r, put_s, loc_s, put_r,
):
    n_mat, tokens, rows = a.shape
    cols = g.shape[2]
    half = rows // 2
    part = half // Q
    per_mat = cols // FB
    steps = n_mat * per_mat
    units = 2 * steps

    me = lax.axis_index("dp")
    z, core = me // 2, me % 2
    middle = (z + 1) // 2 == 1
    end = jnp.logical_not(middle)
    sibling = z * 2 + 1 - core
    partner = (z + 1 - 2 * (z % 2)) * 2 + core
    across = (3 - z) * 2 + core
    mine = pl.multiple_of(core * half, half)

    def a_copy(n, s):
        first = pl.multiple_of((core * s + (1 - core) * (1 - s)) * half, half)
        return pltpu.make_async_copy(a.at[n, :, pl.ds(first, half)], abuf.at[s], a_sem.at[s])

    def g_copy(i):
        n, j = i // per_mat, i % per_mat
        return pltpu.make_async_copy(
            g.at[n, :, pl.ds(pl.multiple_of(j * FB, FB), FB)], gbuf.at[i % 2], g_sem.at[i % 2]
        )

    def g_first(h):
        c = pl.ds(h * UB, UB)
        return pltpu.make_async_copy(g.at[0, :, c], gbuf.at[0, :, c], g_sem.at[2 + h])

    def send(src, dst, s, r, device):
        return pltpu.make_async_remote_copy(
            src_ref=src, dst_ref=dst, send_sem=s, recv_sem=r, device_id={"dp": device}, device_id_type=MESH
        )

    def place(u, q):
        n, col = u // (2 * per_mat), u % (2 * per_mat)
        return out.at[n, pl.ds(mine + q * part, part), pl.ds(pl.multiple_of(col * UB, UB), UB)]

    def piece(q):
        return pl.ds(q * part, part)

    def sib_copy(u):
        return send(sib_out.at[u % 4], sib_in.at[u % 4], sib_s.at[u % 4], sib_r.at[u % 4], sibling)

    def low_copy(u, q):
        v = low.at[u % R, piece(q)]
        return send(v, v, low_s.at[u % R, q], low_r.at[u % R, q], partner)

    def pair_copy(u, q):
        return send(
            pair_out.at[u % S, piece(q)], pair_in.at[u % S, piece(q)],
            pair_s.at[u % S, q], pair_r.at[u % S, q], across,
        )

    def fin_copy(u, q):
        return send(fin.at[u % S, piece(q)], place(u, q), fin_s.at[u % S, q], fin_r.at[u % R, q], partner)

    def loc_copy(u, q):
        return pltpu.make_async_copy(fin.at[u % S, piece(q)], place(u, q), loc_s.at[u % S, q])

    def put_copy(u, q):
        return send(fin.at[u % S, piece(q)], place(u, q), put_s.at[u % S, q], put_r.at[u, q], sibling)

    def pass_copy(u, q):
        return send(place(u, q), place(u, q), put_s.at[u % S, q], put_r.at[u, q], sibling)

    a_copy(0, 0).start()
    g_first(0).start()
    a_copy(0, 1).start()
    g_first(1).start()

    barrier = pltpu.get_barrier_semaphore()
    for d in (sibling, partner):
        pl.semaphore_signal(barrier, inc=1, device_id={"dp": d}, device_id_type=MESH)

    @pl.when(middle)
    def _():
        pl.semaphore_signal(barrier, inc=1, device_id={"dp": across}, device_id_type=MESH)
        pl.semaphore_wait(barrier, 3)

    @pl.when(end)
    def _():
        pl.semaphore_wait(barrier, 2)

    def dot(x, y):
        return lax.dot_general(x, y, (((0,), (0,)), ((), ())), preferred_element_type=jnp.float32)

    def to_sibling(u, d):
        sib_out[u % 4] = d.astype(jnp.bfloat16)
        sib_copy(u).start()

    def chip_sum(u):
        sib_copy(u).wait()

        @pl.when(middle)
        def _():
            own[u % OWN] += sib_in[u % 4].astype(jnp.float32)

        @pl.when(end)
        def _():
            for q in range(Q):
                p = piece(q)
                low[u % R, p] = (own[u % OWN, p] + sib_in[u % 4, p].astype(jnp.float32)).astype(jnp.bfloat16)
                low_copy(u, q).start()

    def piece_c(u, q):
        p = piece(q)
        low_copy(u, q).wait_recv()
        pair_out[u % S, p] = (own[u % OWN, p] + low[u % R, p].astype(jnp.float32)).astype(jnp.bfloat16)
        pair_copy(u, q).start()

    def piece_d(u, q):
        @pl.when(u >= KEEP)
        def _():
            finish_piece(u - KEEP, q)

        p = piece(q)
        pair_copy(u, q).wait()
        fin[u % S, p] = (
            pair_out[u % S, p].astype(jnp.float32) + pair_in[u % S, p].astype(jnp.float32)
        ).astype(jnp.bfloat16)
        fin_copy(u, q).start()
        put_copy(u, q).start()
        loc_copy(u, q).start()

    def finish_piece(u, q):
        fin_copy(u, q).wait_send()
        put_copy(u, q).wait_send()
        loc_copy(u, q).wait()

    def finish_d(u):
        for q in range(Q):
            finish_piece(u, q)

    def finish_e(u):
        for q in range(Q):
            pass_copy(u, q).wait_send()

    def stage_e(u):
        @pl.when(u >= KEEP)
        def _():
            finish_e(u - KEEP)

        for q in range(Q):
            low_copy(u, q).wait_send()
            fin_copy(u, q).wait_recv()
            pass_copy(u, q).start()

    def within(u):
        return (u >= 0) & (u < units)

    def narrow(k, carry):
        u, s = k // 2, k % 2
        i, h = u // 2, u % 2

        @pl.when(k < 2)
        def _():
            a_copy(0, s).wait()

        @pl.when(k == 0)
        def _():
            g_first(0).wait()

        @pl.when(k == 2)
        def _():
            g_first(1).wait()

        @pl.when((h == 0) & (s == 0) & (i > 0))
        def _():
            g_copy(i).wait()

        d = dot(abuf[s], gbuf[i % 2, :, pl.ds(pl.multiple_of(h * UB, UB), UB)])

        @pl.when((h == 0) & (s == 0))
        def _():
            g_copy(i + 1).start()

        @pl.when(s == 0)
        def _():
            to_sibling(u, d)

        @pl.when(s == 1)
        def _():
            own[u % OWN] = d
            chip_sum(u)

        @pl.when(middle & (k >= PD) & (k < 2 * NP - 1))
        def _():
            piece_d((k - PD) // Q, (k - PD) % Q)

        @pl.when(middle & (k >= PC))
        def _():
            piece_c((k - PC) // Q, (k - PC) % Q)

        return carry

    lax.fori_loop(0, 2 * NP, narrow, 0)

    def tick(t, carry):
        i, k = t // 2, t % 2
        n, j = i // per_mat, i % per_mat

        @pl.when(i < steps)
        def _():
            @pl.when(j == 0)
            def _():
                a_copy(n, k).wait()

            @pl.when(k == 0)
            def _():
                g_copy(i).wait()

                @pl.when(i + 1 < steps)
                def _():
                    g_copy(i + 1).start()

            d = dot(abuf[k], gbuf[i % 2])

            @pl.when((j == per_mat - 1) & (n + 1 < n_mat))
            def _():
                a_copy(n + 1, k).start()

            @pl.when(k == 0)
            def _():
                for h in range(2):
                    to_sibling(2 * i + h, d[:, h * UB : (h + 1) * UB])

            @pl.when(k == 1)
            def _():
                for h in range(2):
                    own[(2 * i + h) % OWN] = d[:, h * UB : (h + 1) * UB]
                for h in range(2):
                    chip_sum(2 * i + h)

        for q in range(Q):

            @pl.when(middle & within(t - LD))
            def _():
                piece_d(t - LD, q)

            @pl.when(middle & within(t - LC))
            def _():
                piece_c(t - LC, q)

        @pl.when(end & within(t - LE))
        def _():
            stage_e(t - LE)

        return carry

    lax.fori_loop(NP, units + LE, tick, 0)

    def each(first, f):
        def step(u, c):
            f(u)
            return c

        lax.fori_loop(first, units, step, 0)

    @pl.when(middle)
    def _():
        each(units - KEEP, finish_d)

    @pl.when(end)
    def _():
        each(units - KEEP, finish_e)

    def sibling_rows(u):
        for q in range(Q):
            put_copy(u, q).wait_recv()

    each(0, sibling_rows)


def local(a, g):
    a, g = a[0], g[0]
    n_mat, tokens, rows = a.shape
    cols = g.shape[2]
    half = rows // 2
    steps = n_mat * (cols // FB)
    bf, f32 = jnp.bfloat16, jnp.float32

    def ring(slots, dtype=bf):
        return pltpu.VMEM((slots, half, UB), dtype)

    dma = pltpu.SemaphoreType.DMA
    return pl.pallas_call(
        kernel,
        out_shape=pltpu.VMEM((n_mat, rows, cols), bf),
        in_specs=[pl.BlockSpec(memory_space=pl.ANY)] * 2,
        out_specs=pl.BlockSpec(memory_space=pl.ANY),
        scratch_shapes=[
            pltpu.VMEM((2, tokens, half), bf),
            pltpu.VMEM((2, tokens, FB), bf),
            ring(OWN, f32), ring(4), ring(4), ring(R), ring(S), ring(S), ring(S),
            dma((2,)), dma((4,)),
            dma((4,)), dma((4,)), dma((R, Q)), dma((R, Q)), dma((S, Q)), dma((S, Q)),
            dma((S, Q)), dma((R, Q)), dma((S, Q)), dma((S, Q)), dma((2 * steps, Q)),
        ],
        compiler_params=pltpu.CompilerParams(
            collective_id=0, has_side_effects=True, vmem_limit_bytes=46_000_000
        ),
    )(a, g)


def solution(mesh):
    assert mesh.shape["dp"] == 8
    both = ("rep", "dp")
    return jax.shard_map(
        local, mesh=mesh, in_specs=(P(both), P(both)), out_specs=P("rep"), check_vma=False
    )
```

time: 902 us -> 240 us (0.27)
  blocking collectives: 732 us -> 0 us
  Pallas kernels: 0 us -> 233 us
  matrix products: 169 us -> 0 us
    dot_general x1 -> x0, blocking collectives: 732 us -> none  [step(): jnp.einsum('rsntd,rsntf->rndf', a, g, preferred_element_type=jnp.float32)]
    pallas_call x0 -> x1, Pallas kernels: none -> 233 us  [local(): pl.pallas_call(kernel, out_shape=pltpu.VMEM((n_mat, rows, cols), bf), in_...]
    dot_general x1 -> x0, matrix products: 169 us -> none  [step(): jnp.einsum('rsntd,rsntf->rndf', a, g, preferred_element_type=jnp.float32)]
where the time goes in v2:
time: 240 us
  Pallas kernels  233 us (97%)
  local copies, waits for them, and re-layouts  6.85 us (3%)
    pallas_call x1, Pallas kernels, local(): pl.pallas_call(kernel, out_shape=pltpu.VMEM((n_mat, rows, cols), bf), in_...  233 us
    unnamed x1, local copies, waits for them, and re-layouts  6.85 us

profile of v2, /device:TPU:0, one launch (start us, length us, event | category | flops | bytes accessed | tf_op | source)
XLA Modules:
  0.0 239.8 jit_solution(17155402426231165911)
XLA Ops:
  0.0 232.9 %shard_map.28 = bf16[4,768,3072]{2,1,0:T(8,128)(2,1)S(1)} custom-call(bf16[4,8192,768]{2,1,0:T(8,128)(2,1)} %bitcast.2, bf16[4,8192,3072]{2,1,0:T(8,128)(2,1)} %bitcast.1.g), custom_call_target="tpu_custom_call" | custom-call | tf_op jit(solution)/shard_map/pallas_call | solution.py:313
  232.9 6.9 %copy.4 = bf16[4,768,3072]{2,1,0:T(8,128)(2,1)} copy(bf16[4,768,3072]{2,1,0:T(8,128)(2,1)S(1)} %shard_map.28) | data formatting | bytes 37748736

commit v3 on v2

--- a/solution.py
+++ b/solution.py
@@ -210,7 +210,7 @@
             own[u % OWN] = d
             chip_sum(u)
 
-        @pl.when(middle & (k >= PD) & (k < 2 * NP - 1))
+        @pl.when(middle & (k >= PD))
         def _():
             piece_d((k - PD) // Q, (k - PD) % Q)
 
@@ -258,15 +258,20 @@
                 for h in range(2):
                     chip_sum(2 * i + h)
 
-        for q in range(Q):
-
-            @pl.when(middle & within(t - LD))
-            def _():
+        @pl.when(middle & within(t - LD))
+        def _():
+            for q in range(Q // 2, Q):
                 piece_d(t - LD, q)
 
-            @pl.when(middle & within(t - LC))
-            def _():
+        @pl.when(middle & within(t - LC))
+        def _():
+            for q in range(Q):
                 piece_c(t - LC, q)
+
+        @pl.when(middle & within(t - LD + 1))
+        def _():
+            for q in range(Q // 2):
+                piece_d(t - LD + 1, q)
 
         @pl.when(end & within(t - LE))
         def _():

time: 240 us -> 238 us (level)
  no operation moved by 1% of the time
where the time goes in v3:
time: 238 us
  Pallas kernels  231 us (97%)
  local copies, waits for them, and re-layouts  6.85 us (3%)
    pallas_call x1, Pallas kernels, local(): pl.pallas_call(kernel, out_shape=pltpu.VMEM((n_mat, rows, cols), bf), in_...  231 us
    unnamed x1, local copies, waits for them, and re-layouts  6.85 us

profile of v3, /device:TPU:0, one launch (start us, length us, event | category | flops | bytes accessed | tf_op | source)
XLA Modules:
  0.0 237.7 jit_solution(15845552020608145296)
XLA Ops:
  0.0 230.9 %shard_map.28 = bf16[4,768,3072]{2,1,0:T(8,128)(2,1)S(1)} custom-call(bf16[4,8192,768]{2,1,0:T(8,128)(2,1)} %bitcast.2, bf16[4,8192,3072]{2,1,0:T(8,128)(2,1)} %bitcast.1.g), custom_call_target="tpu_custom_call" | custom-call | tf_op jit(solution)/shard_map/pallas_call | solution.py:318
  230.9 6.9 %copy.4 = bf16[4,768,3072]{2,1,0:T(8,128)(2,1)} copy(bf16[4,768,3072]{2,1,0:T(8,128)(2,1)S(1)} %shard_map.28) | data formatting | bytes 37748736
